TPU v7x, 32 devices: a whole 2x2x4 slice. The times are simulated.
32 devices in a mesh: parts: 2 (over y), blk: 4 (over z), sub: 2 (over x), rep: 2 (over core).
Axes of the slice: x: 2, y: 2, z: 4, core: 2. Of those that a mesh axis runs over, the one named last changes fastest.
Arguments:
- queries: bfloat16 [128, 32, 128], P(('parts', 'blk', 'sub', 'rep')), parts along dimension 0, may hold values from -1.5 to 1.5
- passages: bfloat16 [512, 128, 128], P(('parts', 'blk')), parts along dimension 0, may hold values from -1.5 to 1.5
- lengths: int32 [512], P(('parts', 'blk')), parts along dimension 0, may hold values from 8 to 128
- slot_of: int32 [512], P('parts'), parts along dimension 0, may hold values from 0 to 255, each once
- candidates: int32 [128, 256], P(('parts', 'blk', 'sub', 'rep')), parts along dimension 0, may hold values from 0 to 255
Outputs:
- score: float32 [128, 256], P(('parts', 'blk', 'sub', 'rep')), parts along dimension 0
- top: float32 [128, 10], P(('parts', 'blk', 'sub', 'rep')), parts along dimension 0
There are 2 independent parts, one for each index of `parts`. A program takes and returns all parts, laid end to end along the dimension named above; each array names one. Nothing has to cross between parts.
Inputs may be any that keep to these rules, and one draw needn't show every extreme that they name: `slot_of`: a permutation; storage row r lies on the blk index r // 64. `candidates`: passage ids, repeats allowed. `lengths`: the live slots of a row are its first ones.
All inputs are finite; a program needn't handle non-finite values.
Results may differ from a plain program's by a relative error of at most 0.0003.
Values may be sent and summed in bfloat16 or wider, within the bound.
No kernel may reach another device: no remote copies, remote signals or barrier semaphores. Data moves between devices by JAX's collectives and lax.ppermute only.
A program may use at most 64 MiB of HBM per device.

v0:
```python
import jax
import jax.numpy as jnp
from jax import lax
from jax.sharding import PartitionSpec as P

TOPN = 10


def score_table(rows_q, passages, lengths):
    queries_here = rows_q.shape[0]
    tokens = rows_q.shape[1]
    width = rows_q.shape[2]
    count = passages.shape[0]
    span = passages.shape[1]
    group = 4
    flat = rows_q.reshape(queries_here * tokens, width)
    blocks = passages.reshape(count // group, group * span, width)
    spans = lengths.reshape(count // group, group)

    def one_block(pair):
        piece, live_count = pair
        similar = lax.dot_general(
            flat, piece, (((1,), (1,)), ((), ())), preferred_element_type=jnp.float32
        )
        similar = similar.reshape(queries_here * tokens, group, span)
        live = lax.broadcasted_iota(jnp.int32, (group, span), 1) < live_count[:, None]
        best = jnp.max(jnp.where(live[None], similar, -1e30), axis=2)
        return jnp.sum(best.reshape(queries_here, tokens, group), axis=1) / tokens

    table = lax.map(one_block, (blocks, spans))
    return jnp.transpose(table, (1, 0, 2)).reshape(queries_here, count)


def shards(queries, passages, lengths, slot_of, candidates):
    table = score_table(lax.all_gather(queries, "blk", axis=0, tiled=True), passages, lengths)
    whole = lax.all_to_all(table, "blk", split_axis=0, concat_axis=1, tiled=True)
    score = jnp.take_along_axis(whole, jnp.take(slot_of, candidates, axis=0), axis=1)
    top = lax.top_k(score, TOPN)[0]
    return (score, top)


def solution(mesh):
    return jax.shard_map(
        shards,
        mesh=mesh,
        in_specs=(
            P(("parts", "blk", "sub", "rep"), None, None),
            P(("parts", "blk"), None, None),
            P(("parts", "blk")),
            P("parts"),
            P(("parts", "blk", "sub", "rep"), None),
        ),
        out_specs=(
            P(("parts", "blk", "sub", "rep"), None),
            P(("parts", "blk", "sub", "rep"), None),
        ),
        check_vma=False,
    )
```

profile of v0, /device:TPU:0, one launch (start us, length us, event | category | flops | bytes accessed | tf_op | source)
XLA Modules:
  0.0 66.2 jit_solution(11829611261535838261)
XLA Ops:
  0.7 0.7 %reshape.67 = s32[16,4]{1,0:T(8,128)S(1)} reshape(s32[64]{0:T(128)} %param.9) | data formatting | bytes 512 | tf_op jit(solution)/shard_map/reshape | solution.py:18
  1.4 15.3 %all_gather.3 = bf16[16,32,128]{2,1,0:T(8,128)(2,1)S(1)} all-gather(bf16[4,32,128]{2,1,0:T(8,128)(2,1)} %param.7), channel_id=1, replica_groups=mesh['parts'=2,'blk'=4,'sub'=2,'rep'=2] {'blk'}, dimensions={0}, use_global_device_ids=true | all-gather | bytes 163840 | tf_op jit(solution)/shard_map/all_gather | solution.py:35
  16.7 24.2 %while.10 = (s32[]{:T(128)}, f32[16,16,4]{1,2,0:T(4,128)S(1)}, s32[16,4]{1,0:T(8,128)S(1)}, bf16[16,512,128]{2,1,0:T(8,128)(2,1)}, bf16[512,128]{1,0:T(8,128)(2,1)S(1)}, /*index=5*/s32[]{:T(128)}, f32[]{:T(128)}) while((s32[]{:T(128)}, f32[16,16,4]{1,2,0:T(4,128)S(1)}, s32[16,4]{1,0:T(8,128)S(1)}, bf16[16,512,128]{2,1,0:T(8,128)(2,1)}, ...), condition=%wide.region_3.4_spmd, body=%wide.region_0.3_spmd.sunk | while | flops 67633664 | bytes 300437 | solution.py:30
  16.7 0.1 iota_compare_fusion.2
  16.8 1.2 %select_reduce_fusion.2 = f32[512,4]{0,1:T(4,128)S(1)} fusion(pred[4,128]{1,0:T(4,128)(4,1)S(1)} %iota_compare_fusion.2, bf16[512,128]{1,0:T(8,128)(2,1)S(1)} %get-tuple-element.93, bf16[16,512,128]{2,1,0:T(8,128)(2,1)} %get-tuple-element.92, s32[]{:T(128)S(6)} %copy.17), kind=kOutput, calls=%fused_computation.2.clone.1 | convolution fusion | flops 67631104 | bytes 270852 | tf_op jit(solution)/shard_map/while/body/eval_jaxpr/dot_general | solution.py:22
  18.0 0.1 reshape.95
  18.1 0.1 reduce_sum.10
  18.2 0.1 iota_compare_fusion.2
  18.3 1.2 %select_reduce_fusion.2 = f32[512,4]{0,1:T(4,128)S(1)} fusion(pred[4,128]{1,0:T(4,128)(4,1)S(1)} %iota_compare_fusion.2, bf16[512,128]{1,0:T(8,128)(2,1)S(1)} %get-tuple-element.93, bf16[16,512,128]{2,1,0:T(8,128)(2,1)} %get-tuple-element.92, s32[]{:T(128)S(6)} %copy.17), kind=kOutput, calls=%fused_computation.2.clone.1 | convolution fusion | flops 67631104 | bytes 270852 | tf_op jit(solution)/shard_map/while/body/eval_jaxpr/dot_general | solution.py:22
  19.5 0.1 reshape.95
  19.6 0.1 reduce_sum.10
  19.8 1.2 %select_reduce_fusion.2 = f32[512,4]{0,1:T(4,128)S(1)} fusion(pred[4,128]{1,0:T(4,128)(4,1)S(1)} %iota_compare_fusion.2, bf16[512,128]{1,0:T(8,128)(2,1)S(1)} %get-tuple-element.93, bf16[16,512,128]{2,1,0:T(8,128)(2,1)} %get-tuple-element.92, s32[]{:T(128)S(6)} %copy.17), kind=kOutput, calls=%fused_computation.2.clone.1 | convolution fusion | flops 67631104 | bytes 270852 | tf_op jit(solution)/shard_map/while/body/eval_jaxpr/dot_general | solution.py:22
  21.0 0.1 reshape.95
  21.1 0.1 reduce_sum.10
  21.3 1.2 %select_reduce_fusion.2 = f32[512,4]{0,1:T(4,128)S(1)} fusion(pred[4,128]{1,0:T(4,128)(4,1)S(1)} %iota_compare_fusion.2, bf16[512,128]{1,0:T(8,128)(2,1)S(1)} %get-tuple-element.93, bf16[16,512,128]{2,1,0:T(8,128)(2,1)} %get-tuple-element.92, s32[]{:T(128)S(6)} %copy.17), kind=kOutput, calls=%fused_computation.2.clone.1 | convolution fusion | flops 67631104 | bytes 270852 | tf_op jit(solution)/shard_map/while/body/eval_jaxpr/dot_general | solution.py:22
  22.6 0.1 reshape.95
  22.6 0.1 reduce_sum.10
  22.8 1.2 %select_reduce_fusion.2 = f32[512,4]{0,1:T(4,128)S(1)} fusion(pred[4,128]{1,0:T(4,128)(4,1)S(1)} %iota_compare_fusion.2, bf16[512,128]{1,0:T(8,128)(2,1)S(1)} %get-tuple-element.93, bf16[16,512,128]{2,1,0:T(8,128)(2,1)} %get-tuple-element.92, s32[]{:T(128)S(6)} %copy.17), kind=kOutput, calls=%fused_computation.2.clone.1 | convolution fusion | flops 67631104 | bytes 270852 | tf_op jit(solution)/shard_map/while/body/eval_jaxpr/dot_general | solution.py:22
  24.1 0.1 reshape.95
  24.2 0.1 reduce_sum.10
  24.4 1.2 %select_reduce_fusion.2 = f32[512,4]{0,1:T(4,128)S(1)} fusion(pred[4,128]{1,0:T(4,128)(4,1)S(1)} %iota_compare_fusion.2, bf16[512,128]{1,0:T(8,128)(2,1)S(1)} %get-tuple-element.93, bf16[16,512,128]{2,1,0:T(8,128)(2,1)} %get-tuple-element.92, s32[]{:T(128)S(6)} %copy.17), kind=kOutput, calls=%fused_computation.2.clone.1 | convolution fusion | flops 67631104 | bytes 270852 | tf_op jit(solution)/shard_map/while/body/eval_jaxpr/dot_general | solution.py:22
  25.6 0.1 reshape.95
  25.7 0.1 reduce_sum.10
  25.9 1.2 %select_reduce_fusion.2 = f32[512,4]{0,1:T(4,128)S(1)} fusion(pred[4,128]{1,0:T(4,128)(4,1)S(1)} %iota_compare_fusion.2, bf16[512,128]{1,0:T(8,128)(2,1)S(1)} %get-tuple-element.93, bf16[16,512,128]{2,1,0:T(8,128)(2,1)} %get-tuple-element.92, s32[]{:T(128)S(6)} %copy.17), kind=kOutput, calls=%fused_computation.2.clone.1 | convolution fusion | flops 67631104 | bytes 270852 | tf_op jit(solution)/shard_map/while/body/eval_jaxpr/dot_general | solution.py:22
  27.1 0.1 reshape.95
  27.2 0.1 reduce_sum.10
  27.4 1.2 %select_reduce_fusion.2 = f32[512,4]{0,1:T(4,128)S(1)} fusion(pred[4,128]{1,0:T(4,128)(4,1)S(1)} %iota_compare_fusion.2, bf16[512,128]{1,0:T(8,128)(2,1)S(1)} %get-tuple-element.93, bf16[16,512,128]{2,1,0:T(8,128)(2,1)} %get-tuple-element.92, s32[]{:T(128)S(6)} %copy.17), kind=kOutput, calls=%fused_computation.2.clone.1 | convolution fusion | flops 67631104 | bytes 270852 | tf_op jit(solution)/shard_map/while/body/eval_jaxpr/dot_general | solution.py:22
  28.6 0.1 reshape.95
  28.7 0.1 reduce_sum.10
  28.9 1.2 %select_reduce_fusion.2 = f32[512,4]{0,1:T(4,128)S(1)} fusion(pred[4,128]{1,0:T(4,128)(4,1)S(1)} %iota_compare_fusion.2, bf16[512,128]{1,0:T(8,128)(2,1)S(1)} %get-tuple-element.93, bf16[16,512,128]{2,1,0:T(8,128)(2,1)} %get-tuple-element.92, s32[]{:T(128)S(6)} %copy.17), kind=kOutput, calls=%fused_computation.2.clone.1 | convolution fusion | flops 67631104 | bytes 270852 | tf_op jit(solution)/shard_map/while/body/eval_jaxpr/dot_general | solution.py:22
  30.1 0.1 reshape.95
  30.2 0.1 reduce_sum.10
  30.4 1.2 %select_reduce_fusion.2 = f32[512,4]{0,1:T(4,128)S(1)} fusion(pred[4,128]{1,0:T(4,128)(4,1)S(1)} %iota_compare_fusion.2, bf16[512,128]{1,0:T(8,128)(2,1)S(1)} %get-tuple-element.93, bf16[16,512,128]{2,1,0:T(8,128)(2,1)} %get-tuple-element.92, s32[]{:T(128)S(6)} %copy.17), kind=kOutput, calls=%fused_computation.2.clone.1 | convolution fusion | flops 67631104 | bytes 270852 | tf_op jit(solution)/shard_map/while/body/eval_jaxpr/dot_general | solution.py:22
  31.7 0.1 reshape.95
  31.7 0.1 reduce_sum.10
  31.9 1.2 %select_reduce_fusion.2 = f32[512,4]{0,1:T(4,128)S(1)} fusion(pred[4,128]{1,0:T(4,128)(4,1)S(1)} %iota_compare_fusion.2, bf16[512,128]{1,0:T(8,128)(2,1)S(1)} %get-tuple-element.93, bf16[16,512,128]{2,1,0:T(8,128)(2,1)} %get-tuple-element.92, s32[]{:T(128)S(6)} %copy.17), kind=kOutput, calls=%fused_computation.2.clone.1 | convolution fusion | flops 67631104 | bytes 270852 | tf_op jit(solution)/shard_map/while/body/eval_jaxpr/dot_general | solution.py:22
  33.2 0.1 reshape.95
  33.2 0.1 reduce_sum.10
  33.5 1.2 %select_reduce_fusion.2 = f32[512,4]{0,1:T(4,128)S(1)} fusion(pred[4,128]{1,0:T(4,128)(4,1)S(1)} %iota_compare_fusion.2, bf16[512,128]{1,0:T(8,128)(2,1)S(1)} %get-tuple-element.93, bf16[16,512,128]{2,1,0:T(8,128)(2,1)} %get-tuple-element.92, s32[]{:T(128)S(6)} %copy.17), kind=kOutput, calls=%fused_computation.2.clone.1 | convolution fusion | flops 67631104 | bytes 270852 | tf_op jit(solution)/shard_map/while/body/eval_jaxpr/dot_general | solution.py:22
  34.7 0.1 reshape.95
  34.8 0.1 reduce_sum.10
  35.0 1.2 %select_reduce_fusion.2 = f32[512,4]{0,1:T(4,128)S(1)} fusion(pred[4,128]{1,0:T(4,128)(4,1)S(1)} %iota_compare_fusion.2, bf16[512,128]{1,0:T(8,128)(2,1)S(1)} %get-tuple-element.93, bf16[16,512,128]{2,1,0:T(8,128)(2,1)} %get-tuple-element.92, s32[]{:T(128)S(6)} %copy.17), kind=kOutput, calls=%fused_computation.2.clone.1 | convolution fusion | flops 67631104 | bytes 270852 | tf_op jit(solution)/shard_map/while/body/eval_jaxpr/dot_general | solution.py:22
  36.2 0.1 reshape.95
  36.3 0.1 reduce_sum.10
  36.5 1.2 %select_reduce_fusion.2 = f32[512,4]{0,1:T(4,128)S(1)} fusion(pred[4,128]{1,0:T(4,128)(4,1)S(1)} %iota_compare_fusion.2, bf16[512,128]{1,0:T(8,128)(2,1)S(1)} %get-tuple-element.93, bf16[16,512,128]{2,1,0:T(8,128)(2,1)} %get-tuple-element.92, s32[]{:T(128)S(6)} %copy.17), kind=kOutput, calls=%fused_computation.2.clone.1 | convolution fusion | flops 67631104 | bytes 270852 | tf_op jit(solution)/shard_map/while/body/eval_jaxpr/dot_general | solution.py:22
  37.7 0.1 reshape.95
  37.8 0.1 reduce_sum.10
  38.0 1.2 %select_reduce_fusion.2 = f32[512,4]{0,1:T(4,128)S(1)} fusion(pred[4,128]{1,0:T(4,128)(4,1)S(1)} %iota_compare_fusion.2, bf16[512,128]{1,0:T(8,128)(2,1)S(1)} %get-tuple-element.93, bf16[16,512,128]{2,1,0:T(8,128)(2,1)} %get-tuple-element.92, s32[]{:T(128)S(6)} %copy.17), kind=kOutput, calls=%fused_computation.2.clone.1 | convolution fusion | flops 67631104 | bytes 270852 | tf_op jit(solution)/shard_map/while/body/eval_jaxpr/dot_general | solution.py:22
  39.2 0.1 reshape.95
  39.3 0.1 reduce_sum.10
  39.5 1.2 %select_reduce_fusion.2 = f32[512,4]{0,1:T(4,128)S(1)} fusion(pred[4,128]{1,0:T(4,128)(4,1)S(1)} %iota_compare_fusion.2, bf16[512,128]{1,0:T(8,128)(2,1)S(1)} %get-tuple-element.93, bf16[16,512,128]{2,1,0:T(8,128)(2,1)} %get-tuple-element.92, s32[]{:T(128)S(6)} %copy.17), kind=kOutput, calls=%fused_computation.2.clone.1 | convolution fusion | flops 67631104 | bytes 270852 | tf_op jit(solution)/shard_map/while/body/eval_jaxpr/dot_general | solution.py:22
  40.7 0.1 reshape.95
  40.8 0.1 reduce_sum.10
  40.9 0.1 reshape.91
  41.1 0.1 copy.11
  41.2 0.7 %reshape.92 = f32[4,1,256]{2,1,0:T(1,128)} reshape(f32[4,4,64]{2,1,0:T(4,128)S(1)} %copy.11) | data formatting | bytes 8192
  41.9 5.0 %all-to-all-start = ((f32[4,1,256]{2,1,0:T(1,128)}), f32[4,1,256]{2,1,0:T(1,128)S(1)}, u32[]{:S(2)}, u32[]{:S(2)}) async-start(f32[4,1,256]{2,1,0:T(1,128)} %reshape.92), calls=%async_computation | async-start | bytes 8192 | tf_op jit(solution)/shard_map/all_to_all | solution.py:36
  46.9 6.8 %gather_fusion = s32[1024]{0:T(1024)S(1)} fusion(s32[256]{0:T(256)S(1)} %copy-done, s32[1024]{0:T(1024)S(1)} %broadcast_clamp_fusion), kind=kCustom, calls=%fused_computation | custom fusion | bytes 12288 | tf_op jit(solution)/shard_map/jit(_take)/gather | solution.py:37
  53.8 0.5 broadcast.70
  54.3 0.7 %reduce = f32[4,256]{1,0:T(4,128)S(1)} reduce(f32[4,1,256]{2,1,0:T(1,128)S(1)} %all-to-all-done, f32[]{:T(128)} %broadcast.70), dimensions={1}, to_apply=%all_to_all.15.reduce_sub_computation | reduce | bytes 8196 | tf_op jit(solution)/shard_map/all_to_all | solution.py:36
  54.9 0.1 reshape.93
  55.0 0.1 all_to_all.17
  55.1 9.1 %gather_fusion.1 = f32[1024]{0:T(1024)S(1)} fusion(f32[4,256]{1,0:T(4,128)S(1)} %all_to_all.17, s32[1024]{0:T(1024)S(1)} %bitcast.43), kind=kCustom, calls=%fused_computation.1 | custom fusion | bytes 16384 | tf_op jit(solution)/shard_map/jit(take_along_axis)/gather | solution.py:37
  64.3 1.9 %sort_prefixfusion = f32[4,10]{1,0:T(4,128)} fusion(f32[4,256]{1,0:T(4,128)S(1)} %and_select_fusion), kind=kCustom, calls=%top_k.9.sort_prefix | custom fusion | flops 10240 | bytes 4256 | tf_op jit(solution)/shard_map/top_k | solution.py:38
  (63 shorter events, 1.5 us)
Async XLA Ops:
  0.6 46.2 %copy-start = (s32[256]{0:T(256)S(1)}, s32[256]{0:T(256)}, u32[]{:S(2)}) copy-start(s32[256]{0:T(256)} %param.10) | copy-start | bytes 3076
  0.6 46.2 %copy-start.1 = (s32[4,256]{1,0:T(4,128)S(1)}, s32[4,256]{1,0:T(4,128)}, u32[]{:S(2)}) copy-start(s32[4,256]{1,0:T(4,128)} %param.11) | copy-start | bytes 12292
  41.9 11.9 %all-to-all-start = ((f32[4,1,256]{2,1,0:T(1,128)}), f32[4,1,256]{2,1,0:T(1,128)S(1)}, u32[]{:S(2)}, u32[]{:S(2)}) async-start(f32[4,1,256]{2,1,0:T(1,128)} %reshape.92), calls=%async_computation | async-start | bytes 8192 | tf_op jit(solution)/shard_map/all_to_all | solution.py:36
  64.3 1.9 %copy-start.2 = (f32[4,256]{1,0:T(4,128)}, f32[4,256]{1,0:T(4,128)S(1)}, u32[]{:S(2)}) copy-start(f32[4,256]{1,0:T(4,128)S(1)} %and_select_fusion) | copy-start | bytes 12292
where the time goes:
time: 66.7 us; the launch traced here: 66.2 us
  local copies, waits for them, and re-layouts  19.8 us (30%)
  matrix products  19.6 us (29%)
  blocking collectives  15.3 us (23%)
  other arithmetic  5.42 us (8%)
  starting transfers between devices  4.96 us (7%)
  between operations  0.76 us (1%)
    dot_general x16, matrix products, one_block(): lax.dot_general(flat, piece, (((1,), (1,)), ((), ())), preferred_element_...  19.6 us
    all_gather x1, blocking collectives, shards(): lax.all_gather(queries, 'blk', axis=0, tiled=True)  15.3 us
    gather x2, local copies, waits for them, and re-layouts, shards(): jnp.take_along_axis(whole, jnp.take(slot_of, candidates, axis=0), axis=1)  9.13 us
    gather x2, local copies, waits for them, and re-layouts, shards(): jnp.take(slot_of, candidates, axis=0)  6.84 us
    all_to_all x1, starting transfers between devices, shards(): lax.all_to_all(table, 'blk', split_axis=0, concat_axis=1, tiled=True)  4.96 us
    top_k x1, other arithmetic, shards(): top = lax.top_k(score, TOPN)[0]  1.93 us
    reduce_sum x16, other arithmetic, one_block(): return jnp.sum(best.reshape(queries_here, tokens, group), axis=1) / tokens  1.43 us
  transfers between devices with their start and end apart: 1, of which 0 were waited for; matrix products, arithmetic and copies ran while one was open for 10% of the time, Pallas kernels for 0%

commit v1 on v0

v1 whole, which is shorter than its diff:
```python
import functools

import jax
import jax.numpy as jnp
from jax import lax
from jax.experimental import pallas as pl
from jax.experimental.pallas import tpu as pltpu
from jax.sharding import PartitionSpec as P

TOPN = 10
LANES = 128
SUBLANES = 8
LEAST = -1e30
UNITS = 2


def spread(tokens):
    blank = jnp.zeros_like(tokens)
    return jnp.concatenate(
        [jnp.concatenate([tokens, blank], axis=1), jnp.concatenate([blank, tokens], axis=1)], axis=0
    )


def token_best(accs, passages, limits, tokens):
    count, span, _ = passages.shape
    width = tokens.shape[0]
    pairs = count // 2
    slots = len(accs) // UNITS
    rhs = spread(tokens)
    for unit in range(UNITS):
        pltpu.matmul_push_rhs(rhs, staging_register=0, mxu_index=unit, transpose=True)
    slot = lax.broadcasted_iota(jnp.int32, (span, width), 0)
    tops, waiting = [[], []], []

    def drain():
        pair, acc = waiting.pop(0)
        similar = pltpu.matmul_pop(acc)
        for half in range(2):
            index = pair + half * pairs
            live = slot < limits[index : index + 1, :]
            kept = jnp.where(live, similar[:, half * width : (half + 1) * width], LEAST)
            tops[half].append(jnp.max(kept.reshape(span // SUBLANES, SUBLANES, width), axis=0))

    for pair in range(pairs):
        acc = accs[pair % UNITS * slots + pair // UNITS % slots]
        lhs = jnp.concatenate([passages[pair], passages[pair + pairs]], axis=1)
        pltpu.matmul_acc_lhs(acc, lhs, load_staged_rhs=0 if pair < UNITS else None)
        waiting.append((pair, acc))
        if len(waiting) > len(accs) // 2:
            drain()
    while waiting:
        drain()
    group = min(SUBLANES, pairs)
    ordered = tops[0] + tops[1]
    return jnp.concatenate(
        [jnp.max(jnp.stack(ordered[start : start + group]), axis=1) for start in range(0, count, group)], axis=0
    )


def accumulators(span):
    slots = 4 * 256 // span
    return [pltpu.ACC(unit)((span, 256), jnp.float32) for unit in range(UNITS) for _ in range(slots)]


def scores_of(best, queries_here):
    turned = best.T
    tokens = turned.shape[0] // queries_here
    return jnp.sum(turned.reshape(queries_here, tokens, turned.shape[1]), axis=1) / tokens


def lookup(table, index):
    low = index % LANES
    high = index // LANES
    out = jnp.zeros(index.shape, table.dtype)
    for part in range(table.shape[1] // LANES):
        piece = table[:, part * LANES : (part + 1) * LANES]
        found = jnp.take_along_axis(piece, low, axis=1)
        out = jnp.where(high == part, found, out)
    return out


def lookup_wide(table, index):
    return jnp.concatenate(
        [
            lookup(table, index[:, start : start + LANES])
            for start in range(0, index.shape[1], LANES)
        ],
        axis=1,
    )


def own_kernel(lengths, queries, passages, slots, candidates, table, limits, rows, *, queries_here, owners):
    count, span, width = passages.shape
    for index in range(count):
        limits[index : index + 1, :] = jnp.full((1, limits.shape[1]), lengths[index], jnp.int32)
    row = slots[...]
    step = (row // count + (owners - lax.axis_index("blk"))) % owners
    relative = step * count + row % count
    wanted = candidates[...]
    wanted = jnp.concatenate([wanted] * (SUBLANES // queries_here), axis=0)
    rows[...] = lookup_wide(jnp.broadcast_to(relative, (SUBLANES, row.shape[1])), wanted)

    def body(*accs):
        table[...] = scores_of(token_best(accs, passages, limits, queries[...]), queries_here)

    pl.run_scoped(body, *accumulators(span))


def arrived_kernel(queries, passages, limits, table, *, queries_here):
    def body(*accs):
        table[...] = scores_of(token_best(accs, passages, limits, queries[...]), queries_here)

    pl.run_scoped(body, *accumulators(passages.shape[1]))


def finish_kernel(rows, *refs):
    pieces = refs[:-2]
    score, top = refs[-2:]
    queries_here = score.shape[0]
    table = jnp.concatenate([piece[...] for piece in pieces], axis=1)
    table = jnp.concatenate([table] * (SUBLANES // queries_here), axis=0)
    found = lookup_wide(table, rows[...])
    score[...] = found[:queries_here]
    lane = lax.broadcasted_iota(jnp.int32, (SUBLANES, LANES), 1)
    ranked = jnp.zeros((SUBLANES, LANES), jnp.float32)
    taken = jnp.zeros((SUBLANES, 1), jnp.int32)
    for _ in range(TOPN):
        largest = jnp.max(found, axis=1, keepdims=True)
        same = found == largest
        ranked = jnp.where(lane >= taken, largest, ranked)
        taken = taken + jnp.sum(same.astype(jnp.int32), axis=1, keepdims=True)
        found = jnp.where(same, -jnp.inf, found)
    top[...] = ranked[:queries_here, :TOPN]


def near(value):
    return pltpu.with_memory_space_constraint(value, pltpu.VMEM)


def whole(memory=pltpu.VMEM):
    return pl.BlockSpec(memory_space=memory)


def shards(queries, passages, lengths, slot_of, candidates, owners):
    queries_here, tokens, width = queries.shape
    count, span, _ = passages.shape
    flat = queries.reshape(queries_here * tokens, width)
    ids = slot_of.shape[0]
    wanted = candidates.shape[1]

    def shift(value, step):
        pairs = [(index, (index + step) % owners) for index in range(owners)]
        return lax.ppermute(value, "blk", pairs)

    arrived = [shift(flat, step) for step in range(1, owners)]
    flops = 2 * flat.shape[0] * count * span * width
    estimate = pl.CostEstimate(flops=flops, bytes_accessed=2 * passages.size, transcendentals=0)
    piece_shape = pltpu.VMEM((queries_here, count), jnp.float32)
    stored = near(passages)
    own, limits, rows = pl.pallas_call(
        functools.partial(own_kernel, queries_here=queries_here, owners=owners),
        out_shape=(
            piece_shape,
            pltpu.VMEM((count, flat.shape[0]), jnp.int32),
            pltpu.VMEM((SUBLANES, wanted), jnp.int32),
        ),
        in_specs=[whole(pltpu.SMEM), whole(), whole(), whole(), whole()],
        out_specs=(whole(), whole(), whole()),
        cost_estimate=estimate,
        name="own",
    )(lengths, near(flat), stored, near(slot_of.reshape(1, ids)), near(candidates))
    pieces = [own]
    for step in range(1, owners):
        piece = pl.pallas_call(
            functools.partial(arrived_kernel, queries_here=queries_here),
            out_shape=piece_shape,
            in_specs=[whole(), whole(), whole()],
            out_specs=whole(),
            cost_estimate=estimate,
            name="arrived",
        )(near(arrived[step - 1]), stored, near(limits))
        pieces.append(shift(piece, owners - step))
    score, top = pl.pallas_call(
        finish_kernel,
        out_shape=(
            jax.ShapeDtypeStruct((queries_here, wanted), jnp.float32),
            jax.ShapeDtypeStruct((queries_here, TOPN), jnp.float32),
        ),
        in_specs=[whole()] * (1 + owners),
        out_specs=(whole(), whole()),
        name="finish",
    )(near(rows), *[near(piece) for piece in pieces])
    return score, top


def solution(mesh):
    return jax.shard_map(
        functools.partial(shards, owners=mesh.shape["blk"]),
        mesh=mesh,
        in_specs=(
            P(("parts", "blk", "sub", "rep"), None, None),
            P(("parts", "blk"), None, None),
            P(("parts", "blk")),
            P("parts"),
            P(("parts", "blk", "sub", "rep"), None),
        ),
        out_specs=(
            P(("parts", "blk", "sub", "rep"), None),
            P(("parts", "blk", "sub", "rep"), None),
        ),
        check_vma=False,
    )
```

time: 66.7 us -> 26.6 us (0.40)
  matrix products: 19.6 us -> 0 us
  blocking collectives: 15.3 us -> 0 us
  local copies, waits for them, and re-layouts: 19.8 us -> 5.3 us
  Pallas kernels: 0 us -> 5.56 us
  other arithmetic: 5.42 us -> 0 us
  waiting for transfers between devices: 0.01 us -> 5.31 us
  starting transfers between devices: 4.96 us -> 9.43 us
    dot_general x16 -> x0, matrix products: 19.6 us -> none  [one_block(): lax.dot_general(flat, piece, (((1,), (1,)), ((), ())), preferred_element_...]
    gather x4 -> x0, local copies, waits for them, and re-layouts: 16 us -> none  [the longest x2 9.13 us: shards(): jnp.take_along_axis(whole, jnp.take(slot_of, candidates, axis=0), axis=1)]
    all_gather x1 -> x0, blocking collectives: 15.3 us -> none  [shards(): lax.all_gather(queries, 'blk', axis=0, tiled=True)]
    ppermute x0 -> x6, starting transfers between devices: none -> 9.43 us  [shift(): return lax.ppermute(value, 'blk', pairs)]
    pallas_call x0 -> x5, Pallas kernels: none -> 5.56 us  [the longest x3 2.54 us: shards(): pl.pallas_call(functools.partial(arrived_kernel, queries_here=queries_her...]
    ppermute x0 -> x6, waiting for transfers between devices: none -> 5.31 us  [shift(): return lax.ppermute(value, 'blk', pairs)]
    all_to_all x1 -> x0, starting transfers between devices: 4.96 us -> none  [shards(): lax.all_to_all(table, 'blk', split_axis=0, concat_axis=1, tiled=True)]
    unnamed x10, local copies, waits for them, and re-layouts: 0.81 us -> 5.3 us
  transfers between devices with their start and end apart: 1 -> 6, of which waited for: 0 -> 2; matrix products, arithmetic and copies ran while one was open for 10% -> 0% of each run, Pallas kernels for 0% -> 15%
where the time goes in v1:
time: 26.6 us; the launch traced here: 26.3 us
  starting transfers between devices  9.43 us (35%)
  Pallas kernels  5.56 us (21%)
  waiting for transfers between devices  5.31 us (20%)
  local copies, waits for them, and re-layouts  5.3 us (20%)
  between operations  0.68 us (3%)
    ppermute x6, starting transfers between devices, shift(): return lax.ppermute(value, 'blk', pairs)  9.43 us
    ppermute x6, waiting for transfers between devices, shift(): return lax.ppermute(value, 'blk', pairs)  5.31 us
    unnamed x10, local copies, waits for them, and re-layouts  5.3 us
    pallas_call x3, Pallas kernels, shards(): pl.pallas_call(functools.partial(arrived_kernel, queries_here=queries_her...  2.54 us
    pallas_call x1, Pallas kernels, shards(): pl.pallas_call(functools.partial(own_kernel, queries_here=queries_here, o...  1.52 us
    pallas_call x1, Pallas kernels, shards(): pl.pallas_call(finish_kernel, out_shape=(jax.ShapeDtypeStruct((queries_he...  1.5 us
  transfers between devices with their start and end apart: 6, of which 2 were waited for; matrix products, arithmetic and copies ran while one was open for 0% of the time, Pallas kernels for 15%

profile of v1, /device:TPU:0, one launch (start us, length us, event | category | flops | bytes accessed | tf_op | source)
XLA Modules:
  0.0 26.3 jit_solution(12693344327549109977)
XLA Ops:
  0.6 3.1 %collective-permute-start = (bf16[128,128]{1,0:T(8,128)(2,1)}, bf16[128,128]{1,0:T(8,128)(2,1)S(1)}, u32[]{:S(2)}, u32[]{:S(2)}) collective-permute-start(bf16[128,128]{1,0:T(8,128)(2,1)} %bitcast.2), channel_id=1, source_target_pairs={{0,4},{4,8},{8,12},{12,0},{1,5},{5,9},{9,13},{13,1},{2,6},{6,10},{... | collective-permute-start | bytes 98312 | tf_op jit(solution)/shard_map/ppermute | solution.py:153
  3.7 2.6 %collective-permute-start.2 = (bf16[128,128]{1,0:T(8,128)(2,1)}, bf16[128,128]{1,0:T(8,128)(2,1)S(1)}, u32[]{:S(2)}, u32[]{:S(2)}) collective-permute-start(bf16[128,128]{1,0:T(8,128)(2,1)} %bitcast.3), channel_id=1, source_target_pairs={{0,8},{4,12},{8,0},{12,4},{1,9},{5,13},{9,1},{13,5},{2,10},{6,14},... | collective-permute-start | bytes 98312 | tf_op jit(solution)/shard_map/ppermute | solution.py:153
  6.3 1.3 %collective-permute-start.4 = (bf16[128,128]{1,0:T(8,128)(2,1)}, bf16[128,128]{1,0:T(8,128)(2,1)S(1)}, u32[]{:S(2)}, u32[]{:S(2)}) collective-permute-start(bf16[128,128]{1,0:T(8,128)(2,1)} %bitcast.4), channel_id=1, source_target_pairs={{0,12},{4,0},{8,4},{12,8},{1,13},{5,1},{9,5},{13,9},{2,14},{6,2},{... | collective-permute-start | bytes 98312 | tf_op jit(solution)/shard_map/ppermute | solution.py:153
  7.7 0.0 copy-start
  7.7 1.6 %copy-done = bf16[64,128,128]{2,1,0:T(8,128)(2,1)S(1)} copy-done((bf16[64,128,128]{2,1,0:T(8,128)(2,1)S(1)}, bf16[64,128,128]{2,1,0:T(8,128)(2,1)}, u32[]{:S(2)}) %copy-start) | copy-done | bytes 2097176
  9.3 0.0 copy-start.2
  9.3 0.8 %copy-done.2 = bf16[4,32,128]{2,1,0:T(8,128)(2,1)S(1)} copy-done((bf16[4,32,128]{2,1,0:T(8,128)(2,1)S(1)}, bf16[4,32,128]{2,1,0:T(8,128)(2,1)}, u32[]{:S(2)}) %copy-start.2) | copy-done | bytes 32792
  10.0 0.0 copy-start.3
  10.0 0.7 %copy-done.3 = s32[4,256]{1,0:T(4,128)S(1)} copy-done((s32[4,256]{1,0:T(4,128)S(1)}, s32[4,256]{1,0:T(4,128)}, u32[]{:S(2)}) %copy-start.3) | copy-done | bytes 4120
  10.7 0.0 copy-start.4
  10.7 0.7 %copy-done.4 = s32[256]{0:T(256)S(1)} copy-done((s32[256]{0:T(256)S(1)}, s32[256]{0:T(256)}, u32[]{:S(2)}) %copy-start.4) | copy-done | bytes 1048
  11.4 1.5 %own.1 = (f32[4,64]{1,0:T(4,128)S(1)}, s32[64,128]{1,0:T(8,128)S(1)}, s32[8,256]{1,0:T(8,128)S(1)}) custom-call(s32[64]{0:T(128)} %lengths.1, bf16[128,128]{1,0:T(8,128)(2,1)S(1)} %bitcast.5, bf16[64,128,128]{2,1,0:T(8,128)(2,1)S(1)} %copy-done, s32[1,256]{1,0:T(1,128)S(1)} %bitcast.6, s32[4,256]{1,0:T(4,128)S(1)} %copy-done.3), custom_call_target="tpu_custom_call" | custom-call | flops 268435456 | bytes 2097152 | tf_op jit(solution)/shard_map/own/pallas_call | solution.py:160
  12.9 0.0 collective-permute-done.queries
  12.9 0.0 copy-start.1
  12.9 1.6 %copy-done.1 = bf16[64,128,128]{2,1,0:T(8,128)(2,1)S(1)} copy-done((bf16[64,128,128]{2,1,0:T(8,128)(2,1)S(1)}, bf16[64,128,128]{2,1,0:T(8,128)(2,1)}, u32[]{:S(2)}) %copy-start.1) | copy-done | bytes 2097176
  14.5 0.8 %arrived.3 = f32[4,64]{1,0:T(4,128)S(1)} custom-call(bf16[128,128]{1,0:T(8,128)(2,1)S(1)} %collective-permute-done.queries, bf16[64,128,128]{2,1,0:T(8,128)(2,1)S(1)} %copy-done.1, s32[64,128]{1,0:T(8,128)S(1)} %get-tuple-element.7.limits), custom_call_target="tpu_custom_call" | custom-call | flops 268435456 | bytes 2097152 | tf_op jit(solution)/shard_map/arrived/pallas_call | solution.py:174
  15.4 0.5 %collective-permute-start.1 = (f32[4,64]{1,0:T(4,128)S(1)}, f32[4,64]{1,0:T(4,128)S(1)}, u32[]{:S(2)}, u32[]{:S(2)}) collective-permute-start(f32[4,64]{1,0:T(4,128)S(1)} %arrived.3), channel_id=1, source_target_pairs={{0,12},{4,0},{8,4},{12,8},{1,13},{5,1},{9,5},{13,9},{2,14},{6,2},{... | collective-permute-start | bytes 3080 | tf_op jit(solution)/shard_map/ppermute | solution.py:153
  15.9 0.0 collective-permute-done.2.queries
  15.9 0.9 %arrived.4 = f32[4,64]{1,0:T(4,128)S(1)} custom-call(bf16[128,128]{1,0:T(8,128)(2,1)S(1)} %collective-permute-done.2.queries, bf16[64,128,128]{2,1,0:T(8,128)(2,1)S(1)} %copy-done.1, s32[64,128]{1,0:T(8,128)S(1)} %get-tuple-element.7.limits), custom_call_target="tpu_custom_call" | custom-call | flops 268435456 | bytes 2097152 | tf_op jit(solution)/shard_map/arrived/pallas_call | solution.py:174
  16.7 1.8 %collective-permute-start.3 = (f32[4,64]{1,0:T(4,128)S(1)}, f32[4,64]{1,0:T(4,128)S(1)}, u32[]{:S(2)}, u32[]{:S(2)}) collective-permute-start(f32[4,64]{1,0:T(4,128)S(1)} %arrived.4), channel_id=1, source_target_pairs={{0,8},{4,12},{8,0},{12,4},{1,9},{5,13},{9,1},{13,5},{2,10},{6,14},... | collective-permute-start | bytes 3080 | tf_op jit(solution)/shard_map/ppermute | solution.py:153
  18.5 0.0 collective-permute-done.4.queries
  18.5 0.8 %arrived.5 = f32[4,64]{1,0:T(4,128)S(1)} custom-call(bf16[128,128]{1,0:T(8,128)(2,1)S(1)} %collective-permute-done.4.queries, bf16[64,128,128]{2,1,0:T(8,128)(2,1)S(1)} %copy-done.1, s32[64,128]{1,0:T(8,128)S(1)} %get-tuple-element.7.limits), custom_call_target="tpu_custom_call" | custom-call | flops 268435456 | bytes 2097152 | tf_op jit(solution)/shard_map/arrived/pallas_call | solution.py:174
  19.3 0.1 collective-permute-start.5
  19.5 0.0 collective-permute-done.1.refs_1_
  19.5 1.8 %collective-permute-done.3.refs_2_ = f32[4,64]{1,0:T(4,128)S(1)} collective-permute-done((f32[4,64]{1,0:T(4,128)S(1)}, f32[4,64]{1,0:T(4,128)S(1)}, u32[]{:S(2)}, u32[]{:S(2)}) %collective-permute-start.3) | collective-permute-done | bytes 1056 | tf_op jit(solution)/shard_map/ppermute | solution.py:153
  21.3 3.5 %collective-permute-done.5.refs_3_ = f32[4,64]{1,0:T(4,128)S(1)} collective-permute-done((f32[4,64]{1,0:T(4,128)S(1)}, f32[4,64]{1,0:T(4,128)S(1)}, u32[]{:S(2)}, u32[]{:S(2)}) %collective-permute-start.5) | collective-permute-done | bytes 1056 | tf_op jit(solution)/shard_map/ppermute | solution.py:153
  24.8 1.5 %finish.1 = (f32[4,256]{1,0:T(4,128)}, f32[4,10]{1,0:T(4,128)}) custom-call(s32[8,256]{1,0:T(8,128)S(1)} %get-tuple-element.5.rows, f32[4,64]{1,0:T(4,128)S(1)} %get-tuple-element.6.refs_0_, f32[4,64]{1,0:T(4,128)S(1)} %collective-permute-done.1.refs_1_, f32[4,64]{1,0:T(4,128)S(1)} %collective-permute-done.3.refs_2_, f32[4,64]{1,0:T(4,128)S(1)} %collective-permute-done.5.refs_3_), custom_call_target="tpu_custom_call" | custom-call | tf_op jit(solution)/shard_map/finish/pallas_call | solution.py:183
Async XLA Ops:
  0.6 12.3 %collective-permute-start = (bf16[128,128]{1,0:T(8,128)(2,1)}, bf16[128,128]{1,0:T(8,128)(2,1)S(1)}, u32[]{:S(2)}, u32[]{:S(2)}) collective-permute-start(bf16[128,128]{1,0:T(8,128)(2,1)} %bitcast.2), channel_id=1, source_target_pairs={{0,4},{4,8},{8,12},{12,0},{1,5},{5,9},{9,13},{13,1},{2,6},{6,10},{... | collective-permute-start | bytes 98312 | tf_op jit(solution)/shard_map/ppermute | solution.py:153
  3.7 12.1 %collective-permute-start.2 = (bf16[128,128]{1,0:T(8,128)(2,1)}, bf16[128,128]{1,0:T(8,128)(2,1)S(1)}, u32[]{:S(2)}, u32[]{:S(2)}) collective-permute-start(bf16[128,128]{1,0:T(8,128)(2,1)} %bitcast.3), channel_id=1, source_target_pairs={{0,8},{4,12},{8,0},{12,4},{1,9},{5,13},{9,1},{13,5},{2,10},{6,14},... | collective-permute-start | bytes 98312 | tf_op jit(solution)/shard_map/ppermute | solution.py:153
  6.3 12.2 %collective-permute-start.4 = (bf16[128,128]{1,0:T(8,128)(2,1)}, bf16[128,128]{1,0:T(8,128)(2,1)S(1)}, u32[]{:S(2)}, u32[]{:S(2)}) collective-permute-start(bf16[128,128]{1,0:T(8,128)(2,1)} %bitcast.4), channel_id=1, source_target_pairs={{0,12},{4,0},{8,4},{12,8},{1,13},{5,1},{9,5},{13,9},{2,14},{6,2},{... | collective-permute-start | bytes 98312 | tf_op jit(solution)/shard_map/ppermute | solution.py:153
  7.7 1.6 %copy-start = (bf16[64,128,128]{2,1,0:T(8,128)(2,1)S(1)}, bf16[64,128,128]{2,1,0:T(8,128)(2,1)}, u32[]{:S(2)}) copy-start(bf16[64,128,128]{2,1,0:T(8,128)(2,1)} %passages.7) | copy-start | bytes 6291460
  9.3 0.8 %copy-start.2 = (bf16[4,32,128]{2,1,0:T(8,128)(2,1)S(1)}, bf16[4,32,128]{2,1,0:T(8,128)(2,1)}, u32[]{:S(2)}) copy-start(bf16[4,32,128]{2,1,0:T(8,128)(2,1)} %param.5) | copy-start | bytes 98308
  10.0 0.7 %copy-start.3 = (s32[4,256]{1,0:T(4,128)S(1)}, s32[4,256]{1,0:T(4,128)}, u32[]{:S(2)}) copy-start(s32[4,256]{1,0:T(4,128)} %candidates.1) | copy-start | bytes 12292
  10.7 0.7 %copy-start.4 = (s32[256]{0:T(256)S(1)}, s32[256]{0:T(256)}, u32[]{:S(2)}) copy-start(s32[256]{0:T(256)} %param.8) | copy-start | bytes 3076
  12.9 1.6 %copy-start.1 = (bf16[64,128,128]{2,1,0:T(8,128)(2,1)S(1)}, bf16[64,128,128]{2,1,0:T(8,128)(2,1)}, u32[]{:S(2)}) copy-start(bf16[64,128,128]{2,1,0:T(8,128)(2,1)} %passages.7) | copy-start | bytes 6291460
  15.4 4.1 %collective-permute-start.1 = (f32[4,64]{1,0:T(4,128)S(1)}, f32[4,64]{1,0:T(4,128)S(1)}, u32[]{:S(2)}, u32[]{:S(2)}) collective-permute-start(f32[4,64]{1,0:T(4,128)S(1)} %arrived.3), channel_id=1, source_target_pairs={{0,12},{4,0},{8,4},{12,8},{1,13},{5,1},{9,5},{13,9},{2,14},{6,2},{... | collective-permute-start | bytes 3080 | tf_op jit(solution)/shard_map/ppermute | solution.py:153
  16.7 4.5 %collective-permute-start.3 = (f32[4,64]{1,0:T(4,128)S(1)}, f32[4,64]{1,0:T(4,128)S(1)}, u32[]{:S(2)}, u32[]{:S(2)}) collective-permute-start(f32[4,64]{1,0:T(4,128)S(1)} %arrived.4), channel_id=1, source_target_pairs={{0,8},{4,12},{8,0},{12,4},{1,9},{5,13},{9,1},{13,5},{2,10},{6,14},... | collective-permute-start | bytes 3080 | tf_op jit(solution)/shard_map/ppermute | solution.py:153
  19.3 5.4 %collective-permute-start.5 = (f32[4,64]{1,0:T(4,128)S(1)}, f32[4,64]{1,0:T(4,128)S(1)}, u32[]{:S(2)}, u32[]{:S(2)}) collective-permute-start(f32[4,64]{1,0:T(4,128)S(1)} %arrived.5), channel_id=1, source_target_pairs={{0,4},{4,8},{8,12},{12,0},{1,5},{5,9},{9,13},{13,1},{2,6},{6,10},{... | collective-permute-start | bytes 3080 | tf_op jit(solution)/shard_map/ppermute | solution.py:153
